TPU v7x, 256 devices: a whole 4x4x8 slice. The times are simulated.
256 devices in a mesh: grp: 8 (over z), shard: 32 (over y, x, core).
Axes of the slice: x: 4, y: 4, z: 8, core: 2. Of those that a mesh axis runs over, the one named last changes fastest.
Arguments:
- table: float32 [4096, 8, 128], P('shard')
- table_first: float32 [4096, 8, 128], P('shard'), may hold values from -3 to 3
- table_second: float32 [4096, 8, 128], P('shard')
- slot_table: int32 [4096], P('shard'), may hold values from 0 to 25
- touched: int32 [8, 4096], P('grp', 'shard'), may hold values from 0 to 4095, as said below
- emb_grads: bfloat16 [8, 4096, 8, 128], P('grp', 'shard'), may hold values from -6 to 6
- block_slot: int32 [4096], replicated, may hold values from 0 to 4095, as said below
- dense_x: bfloat16 [13, 1048576], P(None, ('grp', 'shard')), may hold values from -6 to 6
- dense_cot: bfloat16 [1048576, 128], P(('grp', 'shard')), may hold values from -0.0625 to 0.0625
- w_one: float32 [13, 512], replicated, may hold values from -1.75 to 1.75
- w_two: float32 [512, 256], replicated, may hold values from -0.25 to 0.25
- w_three: float32 [256, 128], replicated, may hold values from -0.375 to 0.375
- first_one: float32 [13, 512], replicated, may hold values from -3 to 3
- first_two: float32 [512, 256], replicated, may hold values from -3 to 3
- first_three: float32 [256, 128], replicated, may hold values from -3 to 3
- second_one: float32 [13, 512], replicated, may hold values from 0.001 to 0.3
- second_two: float32 [512, 256], replicated, may hold values from 0.001 to 0.3
- second_three: float32 [256, 128], replicated, may hold values from 0.001 to 0.3
Outputs:
- new_table: float32 [4096, 8, 128], P('shard')
- new_table_first: float32 [4096, 8, 128], P('shard')
- new_table_second: float32 [4096, 8, 128], P('shard')
- new_w_one: float32 [13, 512], replicated
- new_w_two: float32 [512, 256], replicated
- new_w_three: float32 [256, 128], replicated
- new_first_one: float32 [13, 512], replicated
- new_first_two: float32 [512, 256], replicated
- new_first_three: float32 [256, 128], replicated
- new_second_one: float32 [13, 512], replicated
- new_second_two: float32 [512, 256], replicated
- new_second_three: float32 [256, 128], replicated
Inputs may be any that keep to these rules, and one draw needn't show every extreme that they name: `touched`: each device's 128 ids are distinct; at most 8 of them have block_slot // 128 equal to any one shard, and in every draw some shard gets exactly 8 from every device. `block_slot`: A permutation of the 4096 slots.
All inputs are finite; a program needn't handle non-finite values.
Results may differ from a plain program's by a relative error of at most 0.0037.
Values may be sent and summed in bfloat16 or wider, within the bound.
No kernel may reach another device: no remote copies, remote signals or barrier semaphores. Data moves between devices by JAX's collectives and lax.ppermute only.
A program may use at most 128 MiB of HBM per device.

v0:
```python
import jax
import jax.numpy as jnp
from jax import lax
from jax.sharding import Mesh
from jax.sharding import PartitionSpec as P

TABLES = 26
CAP = 8
SHARD = ("shard_0", "shard_1", "shard_2")
GRP_SHARD = ("grp", "shard_0", "shard_1", "shard_2")
beta_one = 0.9
beta_two = 0.999
corr_first = 1.0 - 0.9**10
corr_second = 1.0 - 0.999**10
adam_eps = 1e-06
decay_rate = 0.01
learn_rate = 0.1
ratio_eps = 1e-06


def rows_for(lines, count):
    spare = -lines.shape[0] % count
    if not spare:
        return lines
    return jnp.concatenate([lines, jnp.zeros((spare, *lines.shape[1:]), lines.dtype)])


def from_everyone(value, axis):
    copies = jnp.broadcast_to(value, (lax.axis_size(axis), *value.shape))
    return lax.all_to_all(copies, axis, split_axis=0, concat_axis=0, tiled=True)


def in_order(pieces, dim):
    pieces = jnp.moveaxis(pieces, 0, dim)
    shape = pieces.shape
    return pieces.reshape(*shape[:dim], shape[dim] * shape[dim + 1], *shape[dim + 2 :])


def gathered_by_axis(value, axes, dim):
    far, near = axes
    pieces = from_everyone(from_everyone(value, far), near)
    return in_order(pieces.swapaxes(0, 1).reshape(-1, *value.shape), dim)


def cut_along(value, dim, count):
    before, after = (value.shape[:dim], value.shape[dim + 1 :])
    return jnp.moveaxis(value.reshape(*before, count, -1, *after), dim, 0)


def summed_on_arrival(value, axis, dim):
    count = lax.axis_size(axis)
    pieces = lax.all_to_all(cut_along(value, dim, count), axis, 0, 0, tiled=True)
    return jnp.sum(pieces, axis=0)


def summed_rows(value, axes, dim):
    far, near = axes
    pieces = cut_along(value, dim, lax.axis_size(far))
    nearer = summed_on_arrival(pieces, near, dim + 1)
    arrived = lax.all_to_all(nearer, far, split_axis=0, concat_axis=0, tiled=True)
    return arrived.sum(axis=0)


def total_of(value, axes):
    padded = rows_for(value, lax.axis_size(axes[0]) * lax.axis_size(axes[1]))
    whole = gathered_by_axis(summed_rows(padded, axes, 0), axes, 0)
    return lax.slice_in_dim(whole, 0, len(value)).reshape(value.shape)


def packed_total(arrays, axis):
    line, at, finished = (jnp.concatenate([a.reshape(-1) for a in arrays]), 0, [])
    running = total_of(line, axis)
    for a in arrays:
        finished.append(running[at : at + a.size].reshape(a.shape))
        at += a.size
    return tuple(finished)


def silu_slope(pre_value):
    logistic = jax.nn.sigmoid(pre_value)
    return logistic * (1.0 + pre_value * (1.0 - logistic))


def tower_grads(dense_x, dense_cot, w_one, w_two, w_three):
    w_one_bf = w_one.astype(jnp.bfloat16)
    w_two_bf = w_two.astype(jnp.bfloat16)
    w_three_bf = w_three.astype(jnp.bfloat16)
    pre_one = lax.dot_general(
        dense_x, w_one_bf, (((0,), (0,)), ((), ())), preferred_element_type=jnp.float32
    )
    hidden_one = jax.nn.silu(pre_one).astype(jnp.bfloat16)
    pre_two = jnp.dot(hidden_one, w_two_bf, preferred_element_type=jnp.float32)
    hidden_two = jax.nn.silu(pre_two).astype(jnp.bfloat16)
    grad_three = lax.dot_general(
        hidden_two, dense_cot, (((0,), (0,)), ((), ())), preferred_element_type=jnp.float32
    )
    back_two = (
        lax.dot_general(
            dense_cot, w_three_bf, (((1,), (1,)), ((), ())), preferred_element_type=jnp.float32
        )
        * silu_slope(pre_two)
    ).astype(jnp.bfloat16)
    grad_two = lax.dot_general(
        hidden_one, back_two, (((0,), (0,)), ((), ())), preferred_element_type=jnp.float32
    )
    back_one = (
        lax.dot_general(
            back_two, w_two_bf, (((1,), (1,)), ((), ())), preferred_element_type=jnp.float32
        )
        * silu_slope(pre_one)
    ).astype(jnp.bfloat16)
    grad_one = jnp.dot(dense_x, back_one, preferred_element_type=jnp.float32)
    return (grad_one, grad_two, grad_three)


def lamb_dense(weight, first_in, second_in, gradient):
    first_out = beta_one * first_in + (1.0 - beta_one) * gradient
    second_out = beta_two * second_in + (1.0 - beta_two) * gradient * gradient
    update = (
        first_out / corr_first / (jnp.sqrt(second_out / corr_second) + adam_eps)
        + decay_rate * weight
    )
    trust_ratio = jnp.sqrt(jnp.sum(weight * weight)) / (
        jnp.sqrt(jnp.sum(update * update)) + ratio_eps
    )
    return (weight - learn_rate * trust_ratio * update, first_out, second_out)


def body(
    table,
    table_first,
    table_second,
    slot_table,
    touched,
    emb_grads,
    block_slot,
    dense_x,
    dense_cot,
    w_one,
    w_two,
    w_three,
    first_one,
    first_two,
    first_three,
    second_one,
    second_two,
    second_three,
):
    shards = lax.axis_size(SHARD)
    local_blocks = table.shape[0]
    block_rows = table.shape[1]
    emb_width = table.shape[2]
    row_width = block_rows * emb_width
    capacity = CAP
    dense_terms = tower_grads(dense_x, dense_cot, w_one, w_two, w_three)
    table_hot = (slot_table[:, None] == jnp.arange(TABLES, dtype=jnp.int32)[None, :]).astype(
        jnp.float32
    )
    row_weight = jnp.sum(table * table, axis=(1, 2))
    part_weight = jnp.dot(row_weight, table_hot)
    block_ids = touched[0]
    count_touched = block_ids.shape[0]
    grad_rows = emb_grads[0].reshape(count_touched, row_width)
    slot_index = jnp.take(block_slot, block_ids)
    owner_shard = slot_index // local_blocks
    local_row = slot_index % local_blocks
    owner_hot = (owner_shard[:, None] == jnp.arange(shards, dtype=jnp.int32)[None, :]).astype(
        jnp.int32
    )
    bucket_rank = jnp.cumsum(owner_hot, axis=0) - 1
    bucket_place = jnp.sum(owner_hot * bucket_rank, axis=1)
    send_index = owner_shard * capacity + bucket_place
    picker = jnp.arange(shards * capacity, dtype=jnp.int32)[:, None] == send_index[None, :]
    send_rows = jnp.dot(
        picker.astype(jnp.bfloat16), grad_rows, preferred_element_type=jnp.float32
    ).astype(jnp.bfloat16)
    send_local = jnp.where(
        jnp.any(picker, axis=1), jnp.sum(jnp.where(picker, local_row[None, :], 0), axis=1), -1
    )
    send_rows = send_rows.reshape(shards, capacity, row_width)
    send_local = send_local.reshape(shards, capacity)
    recv_rows, recv_local = (
        lax.all_to_all(send_rows, SHARD, split_axis=0, concat_axis=0, tiled=True),
        lax.all_to_all(send_local, SHARD, split_axis=0, concat_axis=0, tiled=True),
    )
    piece_rows = lax.all_gather(recv_rows, "grp", axis=0, tiled=True).reshape(-1, row_width)
    piece_locals = lax.all_gather(recv_local, "grp", axis=0, tiled=True).reshape(-1)
    matches = piece_locals[:, None] == jnp.arange(local_blocks, dtype=jnp.int32)[None, :]
    summed = lax.dot_general(
        matches.astype(jnp.bfloat16),
        piece_rows,
        (((0,), (0,)), ((), ())),
        preferred_element_type=jnp.float32,
    )
    counted = jnp.sum(matches.astype(jnp.float32), axis=0)
    emb_grad = summed.reshape(local_blocks, block_rows, emb_width)
    touched_mask = (counted > 0.5)[:, None, None]
    new_first = jnp.where(
        touched_mask, beta_one * table_first + (1.0 - beta_one) * emb_grad, table_first
    )
    new_second = jnp.where(
        touched_mask, beta_two * table_second + (1.0 - beta_two) * emb_grad * emb_grad, table_second
    )
    update = jnp.where(
        touched_mask,
        new_first / corr_first / (jnp.sqrt(new_second / corr_second) + adam_eps)
        + decay_rate * table,
        0.0,
    )
    row_update = jnp.sum(update * update, axis=(1, 2))
    part_update = jnp.dot(row_update, table_hot)
    merged = packed_total(
        (dense_terms[0], dense_terms[1], dense_terms[2], part_weight, part_update),
        (("grp", "shard_0"), ("shard_1", "shard_2")),
    )
    dense_grads = (merged[0], merged[1], merged[2])
    weight_total = merged[3] / lax.axis_size("grp")
    update_total = merged[4] / lax.axis_size("grp")
    table_ratio = jnp.sqrt(weight_total) / (jnp.sqrt(update_total) + ratio_eps)
    ratio_rows = jnp.dot(table_hot, table_ratio)
    new_table = table - learn_rate * ratio_rows[:, None, None] * update
    layer_one = lamb_dense(w_one, first_one, second_one, dense_grads[0])
    layer_two = lamb_dense(w_two, first_two, second_two, dense_grads[1])
    layer_three = lamb_dense(w_three, first_three, second_three, dense_grads[2])
    return (
        new_table,
        new_first,
        new_second,
        layer_one[0],
        layer_two[0],
        layer_three[0],
        layer_one[1],
        layer_two[1],
        layer_three[1],
        layer_one[2],
        layer_two[2],
        layer_three[2],
    )


def solution(mesh):
    finer = Mesh(
        mesh.devices.reshape(mesh.shape["grp"], 4, 4, 2), ("grp", "shard_0", "shard_1", "shard_2")
    )
    placed = (
        P(SHARD, None, None),
        P(SHARD, None, None),
        P(SHARD, None, None),
        P(SHARD),
        P("grp", SHARD),
        P("grp", SHARD, None, None),
        P(),
        P(None, GRP_SHARD),
        P(GRP_SHARD, None),
        P(),
        P(),
        P(),
        P(),
        P(),
        P(),
        P(),
        P(),
        P(),
    )
    return jax.shard_map(
        body,
        mesh=finer,
        in_specs=placed,
        out_specs=(
            P(SHARD, None, None),
            P(SHARD, None, None),
            P(SHARD, None, None),
            P(),
            P(),
            P(),
            P(),
            P(),
            P(),
            P(),
            P(),
            P(),
        ),
        check_vma=False,
    )
```

profile of v0, /device:TPU:1, one launch (start us, length us, event | category | flops | bytes accessed | tf_op | source)
XLA Modules:
  0.0 203.5 jit_solution(15515118279379365087)
XLA Ops:
  8.0 1.6 gather_fusion
  12.7 19.9 %all_to_all.42 = bf16[32,8,1024]{2,1,0:T(8,128)(2,1)} all-to-all(bf16[32,8,1024]{2,1,0:T(8,128)(2,1)S(1)} %fusion.2), channel_id=1, replica_groups=mesh['grp'=8,'shard_0'=4,'shard_1'=4,'shard_2'=2] {'shard_0','shard_1','..., dimensions={0} | all-to-all | bytes 1048576 | tf_op jit(solution)/shard_map/all_to_all | solution.py:183
  33.6 3.9 %all-to-all-start = ((s32[32,1,8]{2,1,0:T(1,128)}), s32[32,1,8]{2,1,0:T(1,128)S(1)}, u32[]{:S(2)}, u32[]{:S(2)}) async-start(s32[32,1,8]{2,1,0:T(1,128)} %bitcast.11), calls=%async_computation | async-start | bytes 32768 | tf_op jit(solution)/shard_map/all_to_all | solution.py:184
  37.4 2.1 %multiply_reduce_fusion.3 = bf16[128]{0:T(256)(128)(2,1)S(1)} fusion(f32[128,8,128]{2,1,0:T(8,128)} %param.18), kind=kLoop, calls=%fused_computation.37 | loop fusion | flops 262016 | bytes 524544 | tf_op jit(solution)/shard_map/reduce_sum | solution.py:159
  39.5 6.6 %multiply_convert_fusion.1 = (bf16[4096,512]{1,0:T(8,128)(2,1)S(1)}, f32[4096,512]{1,0:T(8,128)}) fusion(bf16[13,4096]{1,0:T(8,128)(2,1)} %param.25, f32[13,512]{1,0:T(8,128)} %param.27), kind=kOutput, calls=%fused_computation.2 | convolution fusion | flops 65018368 | bytes 12716032 | tf_op jit(solution)/shard_map/dot_general | solution.py:88
  47.4 1.7 fusion
  49.1 2.1 %convolution_bitcast_fusion.1 = f32[64,2,8,128]{3,2,1,0:T(8,128)} fusion(bf16[4096,512]{1,0:T(8,128)(2,1)S(1)} %get-tuple-element.102, bf16[4096,256]{1,0:T(8,128)(2,1)S(1)} %fusion), kind=kOutput, calls=%fused_computation.12 | convolution fusion | flops 1073741824 | bytes 6815744 | tf_op jit(solution)/shard_map/dot_general | solution.py:103
  51.2 1.3 convolution_bitcast_fusion
  52.5 7.6 %fusion.3 = f32[13,512]{1,0:T(8,128)S(1)} fusion(bf16[13,4096]{1,0:T(8,128)(2,1)S(1)} %copy-done.18, f32[4096,512]{1,0:T(8,128)} %get-tuple-element.103, bf16[4096,256]{1,0:T(8,128)(2,1)} %copy-done.20, f32[512,256]{1,0:T(8,128)S(1)} %copy-done.1), kind=kOutput, calls=%fused_computation.13 | convolution fusion | flops 1147273216 | bytes 11143168 | tf_op jit(solution)/shard_map/dot_general | solution.py:112
  61.9 2.0 %copy.95 = f32[128,8,128]{0,2,1:T(8,128)} copy(f32[128,8,128]{2,1,0:T(8,128)} %param.20) | data formatting | bytes 1048576 | tf_op args[2]
  63.9 1.3 copy.107
  65.2 24.8 %all-gather = s32[256,1,8]{2,1,0:T(1,128)S(1)} all-gather(s32[32,1,8]{2,1,0:T(1,128)S(1)} %all-to-all-done), channel_id=2, replica_groups=mesh['grp'=8,'shard_0'=4,'shard_1'=4,'shard_2'=2] {'grp'}, dimensions={0}, use_global_device_ids=true | all-gather | bytes 9216 | tf_op jit(solution)/shard_map/all_gather | solution.py:187
  92.1 6.6 %copy.93 = bf16[2048,1024]{0,1:T(8,128)(2,1)} copy(bf16[2048,1024]{1,0:T(8,128)(2,1)} %bitcast.74) | data formatting | bytes 8388608 | tf_op jit(solution)/shard_map/reshape | solution.py:186
  98.6 5.1 %multiply_reduce_fusion.2 = (bf16[128]{0:T(256)(128)(2,1)S(1)}, f32[128,8,128]{0,2,1:T(8,128)}, f32[128,8,128]{0,2,1:T(8,128)}, f32[128,8,128]{0,2,1:T(8,128)}) fusion(f32[128,8,128]{0,2,1:T(8,128)S(1)} %copy.100, pred[128]{0:T(512)(128)(4,1)S(1)} %broadcast_compare_fusion, f32[128,8,128]{0,2,1:T(8,128)S(1)} %copy-done.9, f32[128,8,128]{0,2,1:T(8,128)} %copy.95, ...), kind=kOutput, calls=%fused_computation.33 | convolution fusion | flops 539492224 | bytes 7348608 | tf_op jit(solution)/shard_map/dot_general | solution.py:189
  103.9 2.8 %concatenate.3 = f32[170752]{0:T(1024)S(1)} concatenate(f32[6656]{0:T(1024)S(1)} %reshape.152, f32[131072]{0:T(1024)S(1)} %bitcast.78, f32[32768]{0:T(1024)S(1)} %convolution_bitcast_fusion, f32[26]{0:T(128)S(1)} %convolution_bitcast_fusion.4, f32[26]{0:T(128)S(1)} %convolution_bitcast_fusion.3, f32[204]{0:T(256)S(1)} %broadcast_in_dim.74), dimensions={0} | concatenate | bytes 1366016 | tf_op jit(solution)/shard_map/concatenate | solution.py:25
  107.7 21.0 %all_to_all.43 = f32[8,32,667]{2,1,0:T(8,128)S(1)} all-to-all(f32[8,32,667]{2,1,0:T(8,128)S(1)} %copy.98), channel_id=1, replica_groups=mesh['grp'=8,'shard_0'=4,'shard_1'=4,'shard_2'=2] {'shard_1','shard_2'}, dimensions={0} | all-to-all | bytes 1366016 | tf_op jit(solution)/shard_map/all_to_all | solution.py:52
  130.4 16.4 %all_to_all.44 = f32[32,1,667]{2,1,0:T(1,128)S(1)} all-to-all(f32[32,1,667]{2,1,0:T(1,128)S(1)} %all_to_all.31), channel_id=1, replica_groups=mesh['grp'=8,'shard_0'=4,'shard_1'=4,'shard_2'=2] {'grp','shard_0'}, dimensions={0} | all-to-all | bytes 170752 | tf_op jit(solution)/shard_map/all_to_all | solution.py:60
  147.0 12.3 %all_to_all.45 = f32[32,1,667]{2,1,0:T(1,128)S(1)} all-to-all(f32[32,1,667]{2,1,0:T(1,128)S(1)} %broadcast_in_dim.75), channel_id=1, replica_groups=mesh['grp'=8,'shard_0'=4,'shard_1'=4,'shard_2'=2] {'grp','shard_0'}, dimensions={0} | all-to-all | bytes 170752 | tf_op jit(solution)/shard_map/all_to_all | solution.py:30
  160.2 7.1 %all-to-all-start.5 = ((f32[8,32,667]{2,1,0:T(8,128)}), f32[8,32,667]{2,1,0:T(8,128)S(1)}, u32[]{:S(2)}, u32[]{:S(2)}) async-start(f32[8,32,667]{2,1,0:T(8,128)} %broadcast_in_dim.76), calls=%async_computation.5 | async-start | bytes 1572864 | tf_op jit(solution)/shard_map/all_to_all | solution.py:30
  169.3 10.2 %all-to-all-done.5 = f32[8,32,667]{2,1,0:T(8,128)S(1)} async-done(((f32[8,32,667]{2,1,0:T(8,128)}), f32[8,32,667]{2,1,0:T(8,128)S(1)}, u32[]{:S(2)}, u32[]{:S(2)}) %all-to-all-start.5) | async-done | bytes 683040 | tf_op jit(solution)/shard_map/all_to_all | solution.py:30
  181.5 1.4 slice.32
  182.9 1.3 multiply_subtract_fusion.1
  187.2 2.3 %multiply_reduce_fusion = (f32[]{:T(128)}, f32[]{:T(128)}, f32[512,256]{1,0:T(8,128)S(1)}, f32[512,256]{1,0:T(8,128)S(1)}) fusion(f32[512,256]{1,0:T(8,128)S(1)} %copy-done.1, f32[667,256]{1,0:T(8,128)S(1)} %slice.30, f32[512,256]{1,0:T(8,128)} %param.31, f32[512,256]{1,0:T(8,128)} %param.34), kind=kLoop, calls=%fused_computation.28 | loop fusion | flops 2228222 | bytes 3145736 | tf_op jit(solution)/shard_map/reduce_sum | solution.py:124
  190.9 1.8 multiply_reduce_fusion.4
  (92 shorter events, 21.7 us)
Async XLA Ops:
  7.2 40.2 %copy-start = (bf16[4096,128]{1,0:T(8,128)(2,1)S(1)}, bf16[4096,128]{1,0:T(8,128)(2,1)}, u32[]{:S(2)}) copy-start(bf16[4096,128]{1,0:T(8,128)(2,1)} %param.26) | copy-start | bytes 3145732
  7.2 84.8 %all-gather.3.cloned.1.call-start = ((), (), s32[]{:S(2)}) async-start(), calls=%async_computation.6 | async-start | bytes 4718592 | tf_op jit(solution)/shard_map/all_gather | solution.py:186
  33.6 31.7 %all-to-all-start = ((s32[32,1,8]{2,1,0:T(1,128)}), s32[32,1,8]{2,1,0:T(1,128)S(1)}, u32[]{:S(2)}, u32[]{:S(2)}) async-start(s32[32,1,8]{2,1,0:T(1,128)} %bitcast.11), calls=%async_computation | async-start | bytes 32768 | tf_op jit(solution)/shard_map/all_to_all | solution.py:184
  39.5 6.6 %copy-start.1 = (f32[512,256]{1,0:T(8,128)S(1)}, f32[512,256]{1,0:T(8,128)}, u32[]{:S(2)}) copy-start(f32[512,256]{1,0:T(8,128)} %param.28) | copy-start | bytes 1572868
  46.1 1.3 copy-start.10
  49.1 2.1 %copy-start.20 = (bf16[4096,256]{1,0:T(8,128)(2,1)}, bf16[4096,256]{1,0:T(8,128)(2,1)S(1)}, u32[]{:S(2)}) copy-start(bf16[4096,256]{1,0:T(8,128)(2,1)S(1)} %fusion) | copy-start | bytes 6291460
  51.2 1.3 copy-start.18
  52.5 7.7 %copy-start.19 = (s32[128]{0:T(128)S(1)}, s32[128]{0:T(128)}, u32[]{:S(2)}) copy-start(s32[128]{0:T(128)} %param.21) | copy-start | bytes 1540
  52.5 7.9 %copy-start.2 = (f32[128,8,128]{2,1,0:T(8,128)S(1)}, f32[128,8,128]{2,1,0:T(8,128)}, u32[]{:S(2)}) copy-start(f32[128,8,128]{2,1,0:T(8,128)} %param.18) | copy-start | bytes 1572868
  52.5 8.3 %copy-start.6 = (f32[128,8,128]{2,1,0:T(8,128)S(1)}, f32[128,8,128]{2,1,0:T(8,128)}, u32[]{:S(2)}) copy-start(f32[128,8,128]{2,1,0:T(8,128)} %param.19) | copy-start | bytes 1572868
  60.8 37.8 %copy-start.3 = (f32[128,8,128]{0,2,1:T(8,128)}, f32[128,8,128]{0,2,1:T(8,128)S(1)}, u32[]{:S(2)}) copy-start(f32[128,8,128]{0,2,1:T(8,128)S(1)} %copy.100) | copy-start | bytes 1572868
  92.0 6.6 %copy-start.9 = (f32[128,8,128]{0,2,1:T(8,128)S(1)}, f32[128,8,128]{0,2,1:T(8,128)}, u32[]{:S(2)}) copy-start(f32[128,8,128]{0,2,1:T(8,128)} %copy.92) | copy-start | bytes 1572868
  107.4 59.9 %copy-start.8 = (f32[128,8,128]{0,2,1:T(8,128)S(1)}, f32[128,8,128]{0,2,1:T(8,128)}, u32[]{:S(2)}) copy-start(f32[128,8,128]{0,2,1:T(8,128)} %get-tuple-element.98) | copy-start | bytes 1572868
  107.4 60.9 %copy-start.7 = (f32[128,8,128]{0,2,1:T(8,128)S(1)}, f32[128,8,128]{0,2,1:T(8,128)}, u32[]{:S(2)}) copy-start(f32[128,8,128]{0,2,1:T(8,128)} %get-tuple-element.99) | copy-start | bytes 1572868
  160.2 19.3 %all-to-all-start.5 = ((f32[8,32,667]{2,1,0:T(8,128)}), f32[8,32,667]{2,1,0:T(8,128)S(1)}, u32[]{:S(2)}, u32[]{:S(2)}) async-start(f32[8,32,667]{2,1,0:T(8,128)} %broadcast_in_dim.76), calls=%async_computation.5 | async-start | bytes 1572864 | tf_op jit(solution)/shard_map/all_to_all | solution.py:30
  179.5 5.6 %copy-start.13 = (f32[13,512]{1,0:T(8,128)S(1)}, f32[13,512]{1,0:T(8,128)}, u32[]{:S(2)}) copy-start(f32[13,512]{1,0:T(8,128)} %param.27) | copy-start | bytes 79876
  179.5 5.6 %copy-start.16 = (f32[13,512]{1,0:T(8,128)S(1)}, f32[13,512]{1,0:T(8,128)}, u32[]{:S(2)}) copy-start(f32[13,512]{1,0:T(8,128)} %param.30) | copy-start | bytes 79876
  179.5 5.6 %copy-start.17 = (f32[13,512]{1,0:T(8,128)S(1)}, f32[13,512]{1,0:T(8,128)}, u32[]{:S(2)}) copy-start(f32[13,512]{1,0:T(8,128)} %param.33) | copy-start | bytes 79876
  185.8 10.8 %copy-start.14 = (f32[13,512]{1,0:T(8,128)}, f32[13,512]{1,0:T(8,128)S(1)}, u32[]{:S(2)}) copy-start(f32[13,512]{1,0:T(8,128)S(1)} %get-tuple-element.94) | copy-start | bytes 79876
  185.8 10.8 %copy-start.15 = (f32[13,512]{1,0:T(8,128)}, f32[13,512]{1,0:T(8,128)S(1)}, u32[]{:S(2)}) copy-start(f32[13,512]{1,0:T(8,128)S(1)} %get-tuple-element.95) | copy-start | bytes 79876
  189.5 7.1 %copy-start.4 = (f32[512,256]{1,0:T(8,128)}, f32[512,256]{1,0:T(8,128)S(1)}, u32[]{:S(2)}) copy-start(f32[512,256]{1,0:T(8,128)S(1)} %get-tuple-element.92) | copy-start | bytes 1572868
  189.5 7.1 %copy-start.5 = (f32[512,256]{1,0:T(8,128)}, f32[512,256]{1,0:T(8,128)S(1)}, u32[]{:S(2)}) copy-start(f32[512,256]{1,0:T(8,128)S(1)} %get-tuple-element.93) | copy-start | bytes 1572868
  192.7 3.9 %copy-start.11 = (f32[256,128]{1,0:T(8,128)}, f32[256,128]{1,0:T(8,128)S(1)}, u32[]{:S(2)}) copy-start(f32[256,128]{1,0:T(8,128)S(1)} %get-tuple-element.90) | copy-start | bytes 393220
  192.7 3.9 %copy-start.12 = (f32[256,128]{1,0:T(8,128)}, f32[256,128]{1,0:T(8,128)S(1)}, u32[]{:S(2)}) copy-start(f32[256,128]{1,0:T(8,128)S(1)} %get-tuple-element.91) | copy-start | bytes 393220
Sparse Core Ops, SparseCore 0:
  32.7 54.4 all-gather.2
where the time goes:
time: 204 us; the launch traced here: 203 us
  blocking collectives  94.5 us (46%)
  matrix products  27.5 us (13%)
  local copies, waits for them, and re-layouts  26.3 us (13%)
  between operations  18.6 us (9%)
  other arithmetic  15.3 us (8%)
  starting transfers between devices  11 us (5%)
  waiting for transfers between devices  10.2 us (5%)
    all_gather x1, blocking collectives, body(): lax.all_gather(recv_local, 'grp', axis=0, tiled=True).reshape(-1)  24.8 us
    all_to_all x1, blocking collectives, summed_on_arrival(): lax.all_to_all(cut_along(value, dim, count), axis, 0, 0, tiled=True)  21 us
    all_to_all x1, blocking collectives, body(): lax.all_to_all(send_rows, SHARD, split_axis=0, concat_axis=0, tiled=True)  19.9 us
    all_to_all x1, blocking collectives, summed_rows(): lax.all_to_all(nearer, far, split_axis=0, concat_axis=0, tiled=True)  16.4 us
    all_to_all x1, blocking collectives, from_everyone(): return lax.all_to_all(copies, axis, split_axis=0, concat_axis=0, tiled=True)  12.3 us
    all_to_all x1, waiting for transfers between devices, from_everyone(): return lax.all_to_all(copies, axis, split_axis=0, concat_axis=0, tiled=True)  10.2 us
    unnamed x50, local copies, waits for them, and re-layouts  7.89 us
    dot_general x1, matrix products, tower_grads(): grad_one = jnp.dot(dense_x, back_one, preferred_element_type=jnp.float32)  7.65 us
  transfers between devices with their start and end apart: 3, of which 1 were waited for; matrix products, arithmetic and copies ran while one was open for 16% of the time, Pallas kernels for 0%

commit v1 on v0

--- a/solution.py
+++ b/solution.py
@@ -16,6 +16,11 @@
 decay_rate = 0.01
 learn_rate = 0.1
 ratio_eps = 1e-06
+
+
+def gather_from_all(x, axis, dim):
+    copies = jnp.concatenate([x] * lax.axis_size(axis), axis=dim)
+    return lax.all_to_all(copies, axis, dim, dim, tiled=True)
 
 
 def rows_for(lines, count):
@@ -184,7 +189,7 @@
         lax.all_to_all(send_local, SHARD, split_axis=0, concat_axis=0, tiled=True),
     )
     piece_rows = lax.all_gather(recv_rows, "grp", axis=0, tiled=True).reshape(-1, row_width)
-    piece_locals = lax.all_gather(recv_local, "grp", axis=0, tiled=True).reshape(-1)
+    piece_locals = gather_from_all(recv_local, "grp", 0).reshape(-1)
     matches = piece_locals[:, None] == jnp.arange(local_blocks, dtype=jnp.int32)[None, :]
     summed = lax.dot_general(
         matches.astype(jnp.bfloat16),

time: 204 us -> 194 us (0.951)
  blocking collectives: 94.5 us -> 65.1 us
  waiting for transfers between devices: 10.2 us -> 21.8 us
  starting transfers between devices: 11 us -> 19.2 us
    all_gather x1 -> x0, blocking collectives: 24.8 us -> none  [body(): lax.all_gather(recv_local, 'grp', axis=0, tiled=True).reshape(-1)]
    all_gather x1, waiting for transfers between devices: 0.02 us -> 9.57 us  [body(): lax.all_gather(recv_rows, 'grp', axis=0, tiled=True).reshape(-1, row_width)]
    all_to_all x0 -> x1, starting transfers between devices: none -> 8.19 us  [gather_from_all(): return lax.all_to_all(copies, axis, dim, dim, tiled=True)]
    all_to_all x1, blocking collectives: 21 us -> 17.1 us  [summed_on_arrival(): lax.all_to_all(cut_along(value, dim, count), axis, 0, 0, tiled=True)]
    all_to_all x0 -> x1, waiting for transfers between devices: none -> 2.06 us  [gather_from_all(): return lax.all_to_all(copies, axis, dim, dim, tiled=True)]
    unnamed x50 -> x52, local copies, waits for them, and re-layouts: 7.89 us -> 8.47 us
  transfers between devices with their start and end apart: 3 -> 4, of which waited for: 1 -> 3; matrix products, arithmetic and copies ran while one was open for 16% -> 17% of each run, Pallas kernels for 0% -> 0%
where the time goes in v1:
time: 194 us; the launch traced here: 193 us
  blocking collectives  65.1 us (34%)
  matrix products  27.4 us (14%)
  local copies, waits for them, and re-layouts  27.2 us (14%)
  waiting for transfers between devices  21.8 us (11%)
  starting transfers between devices  19.2 us (10%)
  between operations  18.7 us (10%)
  other arithmetic  14 us (7%)
    all_to_all x1, blocking collectives, body(): lax.all_to_all(send_rows, SHARD, split_axis=0, concat_axis=0, tiled=True)  19.9 us
    all_to_all x1, blocking collectives, summed_on_arrival(): lax.all_to_all(cut_along(value, dim, count), axis, 0, 0, tiled=True)  17.1 us
    all_to_all x1, blocking collectives, summed_rows(): lax.all_to_all(nearer, far, split_axis=0, concat_axis=0, tiled=True)  15.8 us
    all_to_all x1, blocking collectives, from_everyone(): return lax.all_to_all(copies, axis, split_axis=0, concat_axis=0, tiled=True)  12.3 us
    all_to_all x1, waiting for transfers between devices, from_everyone(): return lax.all_to_all(copies, axis, split_axis=0, concat_axis=0, tiled=True)  10.2 us
    all_gather x1, waiting for transfers between devices, body(): lax.all_gather(recv_rows, 'grp', axis=0, tiled=True).reshape(-1, row_width)  9.57 us
    unnamed x52, local copies, waits for them, and re-layouts  8.47 us
    all_to_all x1, starting transfers between devices, gather_from_all(): return lax.all_to_all(copies, axis, dim, dim, tiled=True)  8.19 us
  transfers between devices with their start and end apart: 4, of which 3 were waited for; matrix products, arithmetic and copies ran while one was open for 17% of the time, Pallas kernels for 0%

profile of v1, /device:TPU:1, one launch (start us, length us, event | category | flops | bytes accessed | tf_op | source)
XLA Modules:
  0.0 193.5 jit_solution(2838776021830047038)
XLA Ops:
  8.0 1.6 gather_fusion
  12.7 19.9 %all_to_all.51 = bf16[32,8,1024]{2,1,0:T(8,128)(2,1)} all-to-all(bf16[32,8,1024]{2,1,0:T(8,128)(2,1)S(1)} %fusion.2), channel_id=1, replica_groups=mesh['grp'=8,'shard_0'=4,'shard_1'=4,'shard_2'=2] {'shard_0','shard_1','..., dimensions={0} | all-to-all | bytes 1048576 | tf_op jit(solution)/shard_map/all_to_all | solution.py:188
  33.6 3.9 %all-to-all-start = ((s32[32,1,8]{2,1,0:T(1,128)}), s32[32,1,8]{2,1,0:T(1,128)S(1)}, u32[]{:S(2)}, u32[]{:S(2)}) async-start(s32[32,1,8]{2,1,0:T(1,128)} %bitcast.11), calls=%async_computation | async-start | bytes 32768 | tf_op jit(solution)/shard_map/all_to_all | solution.py:189
  37.5 6.6 %multiply_convert_fusion.1 = (bf16[4096,512]{1,0:T(8,128)(2,1)S(1)}, f32[4096,512]{1,0:T(8,128)}) fusion(bf16[13,4096]{1,0:T(8,128)(2,1)} %param.25, f32[13,512]{1,0:T(8,128)} %param.27), kind=kOutput, calls=%fused_computation.2 | convolution fusion | flops 65018368 | bytes 12716032 | tf_op jit(solution)/shard_map/dot_general | solution.py:93
  45.3 1.7 fusion
  47.0 2.1 %convolution_bitcast_fusion.1 = f32[64,2,8,128]{3,2,1,0:T(8,128)} fusion(bf16[4096,512]{1,0:T(8,128)(2,1)S(1)} %get-tuple-element.90, bf16[4096,256]{1,0:T(8,128)(2,1)S(1)} %fusion), kind=kOutput, calls=%fused_computation.12 | convolution fusion | flops 1073741824 | bytes 6815744 | tf_op jit(solution)/shard_map/dot_general | solution.py:108
  49.1 1.3 convolution_bitcast_fusion
  50.5 7.6 %fusion.3 = f32[13,512]{1,0:T(8,128)S(1)} fusion(bf16[13,4096]{1,0:T(8,128)(2,1)S(1)} %copy-done.18, f32[4096,512]{1,0:T(8,128)} %get-tuple-element.91, bf16[4096,256]{1,0:T(8,128)(2,1)} %copy-done.20, f32[512,256]{1,0:T(8,128)S(1)} %copy-done.1), kind=kOutput, calls=%fused_computation.13 | convolution fusion | flops 1147273216 | bytes 11143168 | tf_op jit(solution)/shard_map/dot_general | solution.py:117
  60.1 8.2 %all-to-all-start.1 = ((s32[8,1,256]{2,1,0:T(1,128)}), s32[8,1,256]{2,1,0:T(1,128)S(1)}, u32[]{:S(2)}, u32[]{:S(2)}) async-start(s32[8,1,256]{2,1,0:T(1,128)} %reshape.176), calls=%async_computation.1 | async-start | bytes 16384 | tf_op jit(solution)/shard_map/all_to_all | solution.py:23
  69.8 2.0 %copy.109 = f32[128,8,128]{0,2,1:T(8,128)} copy(f32[128,8,128]{2,1,0:T(8,128)} %param.20) | data formatting | bytes 1048576 | tf_op args[2]
  71.8 1.3 copy.121
  73.1 2.1 %all-to-all-done.1 = s32[8,1,256]{2,1,0:T(1,128)S(1)} async-done(((s32[8,1,256]{2,1,0:T(1,128)}), s32[8,1,256]{2,1,0:T(1,128)S(1)}, u32[]{:S(2)}, u32[]{:S(2)}) %all-to-all-start.1) | async-done | bytes 8224 | tf_op jit(solution)/shard_map/all_to_all | solution.py:23
  77.0 9.6 %all-gather.2.cloned.1.call-done = bf16[256,8,1024]{2,1,0:T(8,128)(2,1)} async-done(((bf16[32,8,1024]{2,1,0:T(8,128)(2,1)}), bf16[256,8,1024]{2,1,0:T(8,128)(2,1)}) %all-gather.2.cloned.1.call-update) | async-done | bytes 4194320 | tf_op jit(solution)/shard_map/all_gather | solution.py:191
  86.6 6.6 %copy.107 = bf16[2048,1024]{0,1:T(8,128)(2,1)} copy(bf16[2048,1024]{1,0:T(8,128)(2,1)} %bitcast.81) | data formatting | bytes 8388608 | tf_op jit(solution)/shard_map/reshape | solution.py:191
  93.2 5.1 %multiply_reduce_fusion.2 = (bf16[128]{0:T(256)(128)(2,1)S(1)}, f32[128,8,128]{0,2,1:T(8,128)}, f32[128,8,128]{0,2,1:T(8,128)}, f32[128,8,128]{0,2,1:T(8,128)}) fusion(f32[128,8,128]{0,2,1:T(8,128)S(1)} %copy.114, pred[128]{0:T(512)(128)(4,1)S(1)} %broadcast_compare_fusion, f32[128,8,128]{0,2,1:T(8,128)S(1)} %copy-done.9, f32[128,8,128]{0,2,1:T(8,128)} %copy.109, ...), kind=kOutput, calls=%fused_computation.33 | convolution fusion | flops 539492224 | bytes 7348608 | tf_op jit(solution)/shard_map/dot_general | solution.py:194
  98.4 2.8 %concatenate.7 = f32[170752]{0:T(1024)S(1)} concatenate(f32[6656]{0:T(1024)S(1)} %reshape.155, f32[131072]{0:T(1024)S(1)} %bitcast.85, f32[32768]{0:T(1024)S(1)} %convolution_bitcast_fusion, f32[26]{0:T(128)S(1)} %convolution_bitcast_fusion.4, f32[26]{0:T(128)S(1)} %convolution_bitcast_fusion.3, f32[204]{0:T(256)S(1)} %broadcast_in_dim.74), dimensions={0} | concatenate | bytes 1366016 | tf_op jit(solution)/shard_map/concatenate | solution.py:30
  102.2 17.1 %all_to_all.52 = f32[8,32,667]{2,1,0:T(8,128)S(1)} all-to-all(f32[8,32,667]{2,1,0:T(8,128)S(1)} %copy.112), channel_id=1, replica_groups=mesh['grp'=8,'shard_0'=4,'shard_1'=4,'shard_2'=2] {'shard_1','shard_2'}, dimensions={0} | all-to-all | bytes 1366016 | tf_op jit(solution)/shard_map/all_to_all | solution.py:57
  121.0 15.8 %all_to_all.53 = f32[32,1,667]{2,1,0:T(1,128)S(1)} all-to-all(f32[32,1,667]{2,1,0:T(1,128)S(1)} %all_to_all.39), channel_id=1, replica_groups=mesh['grp'=8,'shard_0'=4,'shard_1'=4,'shard_2'=2] {'grp','shard_0'}, dimensions={0} | all-to-all | bytes 170752 | tf_op jit(solution)/shard_map/all_to_all | solution.py:65
  136.9 12.3 %all_to_all.54 = f32[32,1,667]{2,1,0:T(1,128)S(1)} all-to-all(f32[32,1,667]{2,1,0:T(1,128)S(1)} %broadcast_in_dim.75), channel_id=1, replica_groups=mesh['grp'=8,'shard_0'=4,'shard_1'=4,'shard_2'=2] {'grp','shard_0'}, dimensions={0} | all-to-all | bytes 170752 | tf_op jit(solution)/shard_map/all_to_all | solution.py:35
  150.2 7.1 %all-to-all-start.6 = ((f32[8,32,667]{2,1,0:T(8,128)}), f32[8,32,667]{2,1,0:T(8,128)S(1)}, u32[]{:S(2)}, u32[]{:S(2)}) async-start(f32[8,32,667]{2,1,0:T(8,128)} %broadcast_in_dim.76), calls=%async_computation.6 | async-start | bytes 1572864 | tf_op jit(solution)/shard_map/all_to_all | solution.py:35
  159.3 10.2 %all-to-all-done.6 = f32[8,32,667]{2,1,0:T(8,128)S(1)} async-done(((f32[8,32,667]{2,1,0:T(8,128)}), f32[8,32,667]{2,1,0:T(8,128)S(1)}, u32[]{:S(2)}, u32[]{:S(2)}) %all-to-all-start.6) | async-done | bytes 683040 | tf_op jit(solution)/shard_map/all_to_all | solution.py:35
  171.5 1.4 slice.32
  177.2 2.3 %multiply_reduce_fusion = (f32[]{:T(128)}, f32[]{:T(128)}, f32[512,256]{1,0:T(8,128)S(1)}, f32[512,256]{1,0:T(8,128)S(1)}) fusion(f32[512,256]{1,0:T(8,128)S(1)} %copy-done.1, f32[667,256]{1,0:T(8,128)S(1)} %slice.30, f32[512,256]{1,0:T(8,128)} %param.31, f32[512,256]{1,0:T(8,128)} %param.34), kind=kLoop, calls=%fused_computation.28 | loop fusion | flops 2228222 | bytes 3145736 | tf_op jit(solution)/shard_map/reduce_sum | solution.py:129
  180.9 1.8 multiply_reduce_fusion.4
  (100 shorter events, 24.6 us)
Async XLA Ops:
  7.2 38.1 %copy-start = (bf16[4096,128]{1,0:T(8,128)(2,1)S(1)}, bf16[4096,128]{1,0:T(8,128)(2,1)}, u32[]{:S(2)}) copy-start(bf16[4096,128]{1,0:T(8,128)(2,1)} %param.26) | copy-start | bytes 3145732
  7.2 79.4 %all-gather.2.cloned.1.call-start = ((), (), s32[]{:S(2)}) async-start(), calls=%async_computation.7 | async-start | bytes 4718592 | tf_op jit(solution)/shard_map/all_gather | solution.py:191
  33.6 25.6 %all-to-all-start = ((s32[32,1,8]{2,1,0:T(1,128)}), s32[32,1,8]{2,1,0:T(1,128)S(1)}, u32[]{:S(2)}, u32[]{:S(2)}) async-start(s32[32,1,8]{2,1,0:T(1,128)} %bitcast.11), calls=%async_computation | async-start | bytes 32768 | tf_op jit(solution)/shard_map/all_to_all | solution.py:189
  37.4 6.6 %copy-start.1 = (f32[512,256]{1,0:T(8,128)S(1)}, f32[512,256]{1,0:T(8,128)}, u32[]{:S(2)}) copy-start(f32[512,256]{1,0:T(8,128)} %param.28) | copy-start | bytes 1572868
  47.0 2.1 %copy-start.20 = (bf16[4096,256]{1,0:T(8,128)(2,1)}, bf16[4096,256]{1,0:T(8,128)(2,1)S(1)}, u32[]{:S(2)}) copy-start(bf16[4096,256]{1,0:T(8,128)(2,1)S(1)} %fusion) | copy-start | bytes 6291460
  49.1 1.3 copy-start.18
  50.4 7.7 %copy-start.2 = (f32[128,8,128]{2,1,0:T(8,128)S(1)}, f32[128,8,128]{2,1,0:T(8,128)}, u32[]{:S(2)}) copy-start(f32[128,8,128]{2,1,0:T(8,128)} %param.18) | copy-start | bytes 1572868
  50.5 17.8 %copy-start.19 = (s32[128]{0:T(128)S(1)}, s32[128]{0:T(128)}, u32[]{:S(2)}) copy-start(s32[128]{0:T(128)} %param.21) | copy-start | bytes 1540
  50.5 18.2 %copy-start.6 = (f32[128,8,128]{2,1,0:T(8,128)S(1)}, f32[128,8,128]{2,1,0:T(8,128)}, u32[]{:S(2)}) copy-start(f32[128,8,128]{2,1,0:T(8,128)} %param.19) | copy-start | bytes 1572868
  60.1 15.1 %all-to-all-start.1 = ((s32[8,1,256]{2,1,0:T(1,128)}), s32[8,1,256]{2,1,0:T(1,128)S(1)}, u32[]{:S(2)}, u32[]{:S(2)}) async-start(s32[8,1,256]{2,1,0:T(1,128)} %reshape.176), calls=%async_computation.1 | async-start | bytes 16384 | tf_op jit(solution)/shard_map/all_to_all | solution.py:23
  68.7 24.4 %copy-start.3 = (f32[128,8,128]{0,2,1:T(8,128)}, f32[128,8,128]{0,2,1:T(8,128)S(1)}, u32[]{:S(2)}) copy-start(f32[128,8,128]{0,2,1:T(8,128)S(1)} %copy.114) | copy-start | bytes 1572868
  86.6 6.6 %copy-start.9 = (f32[128,8,128]{0,2,1:T(8,128)S(1)}, f32[128,8,128]{0,2,1:T(8,128)}, u32[]{:S(2)}) copy-start(f32[128,8,128]{0,2,1:T(8,128)} %copy.106) | copy-start | bytes 1572868
  102.0 55.3 %copy-start.8 = (f32[128,8,128]{0,2,1:T(8,128)S(1)}, f32[128,8,128]{0,2,1:T(8,128)}, u32[]{:S(2)}) copy-start(f32[128,8,128]{0,2,1:T(8,128)} %get-tuple-element.86) | copy-start | bytes 1572868
  102.0 56.3 %copy-start.7 = (f32[128,8,128]{0,2,1:T(8,128)S(1)}, f32[128,8,128]{0,2,1:T(8,128)}, u32[]{:S(2)}) copy-start(f32[128,8,128]{0,2,1:T(8,128)} %get-tuple-element.87) | copy-start | bytes 1572868
  150.2 19.3 %all-to-all-start.6 = ((f32[8,32,667]{2,1,0:T(8,128)}), f32[8,32,667]{2,1,0:T(8,128)S(1)}, u32[]{:S(2)}, u32[]{:S(2)}) async-start(f32[8,32,667]{2,1,0:T(8,128)} %broadcast_in_dim.76), calls=%async_computation.6 | async-start | bytes 1572864 | tf_op jit(solution)/shard_map/all_to_all | solution.py:35
  169.5 5.6 %copy-start.13 = (f32[13,512]{1,0:T(8,128)S(1)}, f32[13,512]{1,0:T(8,128)}, u32[]{:S(2)}) copy-start(f32[13,512]{1,0:T(8,128)} %param.27) | copy-start | bytes 79876
  169.5 5.6 %copy-start.16 = (f32[13,512]{1,0:T(8,128)S(1)}, f32[13,512]{1,0:T(8,128)}, u32[]{:S(2)}) copy-start(f32[13,512]{1,0:T(8,128)} %param.30) | copy-start | bytes 79876
  169.5 5.6 %copy-start.17 = (f32[13,512]{1,0:T(8,128)S(1)}, f32[13,512]{1,0:T(8,128)}, u32[]{:S(2)}) copy-start(f32[13,512]{1,0:T(8,128)} %param.33) | copy-start | bytes 79876
  175.8 10.8 %copy-start.14 = (f32[13,512]{1,0:T(8,128)}, f32[13,512]{1,0:T(8,128)S(1)}, u32[]{:S(2)}) copy-start(f32[13,512]{1,0:T(8,128)S(1)} %get-tuple-element.82) | copy-start | bytes 79876
  175.8 10.8 %copy-start.15 = (f32[13,512]{1,0:T(8,128)}, f32[13,512]{1,0:T(8,128)S(1)}, u32[]{:S(2)}) copy-start(f32[13,512]{1,0:T(8,128)S(1)} %get-tuple-element.83) | copy-start | bytes 79876
  179.4 7.1 %copy-start.4 = (f32[512,256]{1,0:T(8,128)}, f32[512,256]{1,0:T(8,128)S(1)}, u32[]{:S(2)}) copy-start(f32[512,256]{1,0:T(8,128)S(1)} %get-tuple-element.80) | copy-start | bytes 1572868
  179.4 7.1 %copy-start.5 = (f32[512,256]{1,0:T(8,128)}, f32[512,256]{1,0:T(8,128)S(1)}, u32[]{:S(2)}) copy-start(f32[512,256]{1,0:T(8,128)S(1)} %get-tuple-element.81) | copy-start | bytes 1572868
  182.7 3.9 %copy-start.11 = (f32[256,128]{1,0:T(8,128)}, f32[256,128]{1,0:T(8,128)S(1)}, u32[]{:S(2)}) copy-start(f32[256,128]{1,0:T(8,128)S(1)} %get-tuple-element.78) | copy-start | bytes 393220
  182.7 3.9 %copy-start.12 = (f32[256,128]{1,0:T(8,128)}, f32[256,128]{1,0:T(8,128)S(1)}, u32[]{:S(2)}) copy-start(f32[256,128]{1,0:T(8,128)S(1)} %get-tuple-element.79) | copy-start | bytes 393220
  (1 other events, 1.3 us)
Sparse Core Ops, SparseCore 0:
  32.7 53.8 all-gather.1
